TPU v7x, 32 devices: a whole 2x2x4 slice. The times are simulated.
32 devices in a mesh: rep: 4 (over y, x), col: 8 (over z, core).
Axes of the slice: x: 2, y: 2, z: 4, core: 2. Of those that a mesh axis runs over, the one named last changes fastest.
Arguments:
- tables: float32 [2, 256, 32768], P(None, 'col', 'rep'), may hold values from -4 to 4
- accumulator: float32 [2, 32768], P(None, 'rep'), may hold values from 0.1 to 20
- replica_grads: bfloat16 [4, 2, 256, 16384], P('rep', None, 'col'), may hold values from -6 to 6
- block_ids: int32 [2, 128], replicated, may hold values from 0 to 255, as said below
Outputs:
- new_tables: float32 [2, 256, 32768], P(None, 'col', 'rep')
- new_accumulator: float32 [2, 32768], P(None, 'rep')
Inputs may be any that keep to these rules, and one draw needn't show every extreme that they name: `block_ids`: the block ids of one table are distinct; each names a block of 128 rows. Splitting the 32768 rows into 4 equal runs, each run holds exactly 32 of a table's touched blocks.
All inputs are finite; a program needn't handle non-finite values.
Results may differ from a plain program's by a relative error of at most 0.0003.
Values sent between devices are 32-bit elements; how exact they have to be, the bound alone decides.
A program may use at most 64 MiB of HBM per device.

v0:
```python
import functools
import math

import jax
import jax.numpy as jnp
from jax import lax
from jax.experimental import pallas as pl
from jax.experimental.pallas import tpu as pltpu
from jax.sharding import PartitionSpec as P

BLOCK = 128
MESH = pl.DeviceIdType.MESH
GROUP = 16


def layout(mesh, shape, n_slab):
    reps, cols = mesh.shape["rep"], mesh.shape["col"]
    inner = math.isqrt(reps)
    while reps % inner:
        inner -= 1
    ntab, width, _ = shape
    per = n_slab // BLOCK // reps
    group = math.gcd(per, GROUP)
    return dict(reps=reps, cols=cols, inner=inner, outer=reps // inner, ntab=ntab,
                width=width, per=per, group=group, pieces=per // group)


def pack(cfg, block_ids, grads, packed, ids_out, order_vec, order, order_sem):
    reps, per, group, pieces = cfg["reps"], cfg["per"], cfg["group"], cfg["pieces"]
    ntab, nblk = block_ids.shape
    lane = lax.broadcasted_iota(jnp.int32, (nblk, nblk), 1).astype(jnp.float32)
    slot = lax.broadcasted_iota(jnp.int32, (nblk, nblk), 0).astype(jnp.float32)
    for t in range(ntab):
        across = jnp.broadcast_to(block_ids[pl.ds(t, 1), :].astype(jnp.float32), (nblk, nblk))
        down = across.T
        place = jnp.sum(jnp.where(across < down, 1.0, 0.0), axis=1, keepdims=True)
        hit = place == lane
        order_vec[pl.ds(t, 1), :] = jnp.sum(jnp.where(hit, slot, 0.0), axis=0, keepdims=True).astype(jnp.int32)
        ids_out[pl.ds(t, 1), :] = jnp.sum(jnp.where(hit, down, 0.0), axis=0, keepdims=True).astype(jnp.int32)
    to_scalar = pltpu.make_async_copy(order_vec, order, order_sem)
    to_scalar.start()
    to_scalar.wait()

    def piece(t, g):
        for owner in range(reps):
            for i in range(group):
                at = order[t, owner * per + g * group + i]
                lanes = pl.ds(pl.multiple_of(at * BLOCK, BLOCK), BLOCK)
                packed[t * pieces + g, owner, :, pl.ds(i * BLOCK, BLOCK)] = grads[0, t, :, lanes].astype(jnp.float32)

    for t in range(ntab):
        lax.fori_loop(0, pieces, lambda g, n, t=t: (piece(t, g), n)[1], 0)


def exchange(cfg, packed, total, squares_out, *scratch):
    reps, cols, inner, outer = cfg["reps"], cfg["cols"], cfg["inner"], cfg["outer"]
    ntab, width, per, group = cfg["ntab"], cfg["width"], cfg["per"], cfg["group"]
    pieces = cfg["pieces"]
    (landed, relayed, landed2, sq_all, s1, r1, s2, r2, s3, r3) = scratch
    chunks = ntab * pieces
    me = lax.axis_index("rep")
    my_col = lax.axis_index("col")
    x, y = lax.rem(me, inner), me // inner

    barrier = pltpu.get_barrier_semaphore()
    for f in range(1, inner):
        pl.semaphore_signal(barrier, inc=1, device_id={"rep": y * inner + lax.rem(x + f, inner)}, device_id_type=MESH)
    for f in range(1, outer):
        pl.semaphore_signal(barrier, inc=1, device_id={"rep": lax.rem(y + f, outer) * inner + x}, device_id_type=MESH)
    for f in range(1, cols):
        pl.semaphore_signal(barrier, inc=1, device_id={"col": lax.rem(my_col + f, cols)}, device_id_type=MESH)

    def axes(c):
        return (inner, outer) if c % 2 == 0 else (outer, inner)

    def rank(c, f, s):
        if c % 2 == 0:
            return lax.rem(y + s, outer) * inner + lax.rem(x + f, inner)
        return lax.rem(y + f, outer) * inner + lax.rem(x + s, inner)

    def place(i):
        return pl.ds(pl.multiple_of(i * BLOCK, BLOCK), BLOCK)

    def own(c, owner, i):
        return packed[c, owner, :, place(i)]

    def each(fn):
        lax.fori_loop(0, group, lambda i, n: (fn(i), n)[1], 0, unroll=True)

    def first_copy(c, f, s):
        return pltpu.make_async_remote_copy(
            packed.at[c, rank(c, f, s)], landed.at[c, f - 1, s], s1.at[c, f - 1, s], r1.at[c, f - 1, s],
            device_id={"rep": rank(c, f, 0)}, device_id_type=MESH)

    def second_copy(c, s):
        return pltpu.make_async_remote_copy(
            relayed.at[c, s - 1], landed2.at[c, s - 1], s2.at[c, s - 1], r2.at[c, s - 1],
            device_id={"rep": rank(c, 0, s)}, device_id_type=MESH)

    def square_copy(c, f):
        return pltpu.make_async_remote_copy(
            sq_all.at[c, my_col], sq_all.at[c, my_col], s3.at[c, f - 1], r3.at[c, f - 1],
            device_id={"col": lax.rem(my_col + f, cols)}, device_id_type=MESH)

    def send_far(c):
        nf, ns = axes(c)
        for s in range(1, ns):
            for f in range(1, nf):
                first_copy(c, f, s).start()

    def send_near(c):
        for f in range(1, axes(c)[0]):
            first_copy(c, f, 0).start()

    def relay(c):
        nf, ns = axes(c)
        for s in range(1, ns):
            for f in range(1, nf):
                first_copy(c, f, s).wait_recv()
            owner = rank(c, 0, s)

            def add(i):
                acc = own(c, owner, i)
                for f in range(1, nf):
                    acc = acc + landed[c, f - 1, s, :, place(i)]
                relayed[c, s - 1, :, place(i)] = acc

            each(add)

    def send_relay(c):
        _, ns = axes(c)
        for s in range(1, ns):
            second_copy(c, s).start()

    def finish(c):
        nf, ns = axes(c)
        for f in range(1, nf):
            first_copy(c, f, 0).wait_recv()
        for s in range(1, ns):
            second_copy(c, s).wait_recv()

        def add(i):
            acc = own(c, me, i)
            for f in range(1, nf):
                acc = acc + landed[c, f - 1, 0, :, place(i)]
            for s in range(1, ns):
                acc = acc + landed2[c, s - 1, :, place(i)]
            total[c, :, place(i)] = acc
            sq_all[c, my_col, pl.ds(i, 1), :] = jnp.sum(acc * acc, axis=0, keepdims=True)

        each(add)

    def send_squares(c):
        for f in range(1, cols):
            square_copy(c, f).start()

    def gather_squares(c):
        for f in range(1, cols):
            square_copy(c, f).wait_recv()
        acc = sq_all[c, 0]
        for f in range(1, cols):
            acc = acc + sq_all[c, f]
        squares_out[c] = acc

    pairs = [[c for c in (k, k + 1) if c < chunks] for k in range(0, chunks, 2)]
    steps = len(pairs)

    def at(k, fns):
        if 0 <= k < steps:
            for fn in fns:
                for c in pairs[k]:
                    fn(c)

    greeted = inner - 1 + outer - 1 + cols - 1
    pl.semaphore_wait(barrier, greeted)
    for k in range(steps):
        at(k, [send_far])
    for k in range(steps):
        at(k, [send_near])
    for k in range(steps + 2):
        at(k, [relay, send_relay])
        at(k - 1, [finish, send_squares])
        at(k - 2, [gather_squares])

    for c in range(chunks):
        nf, ns = axes(c)
        for s in range(ns):
            for f in range(1, nf):
                first_copy(c, f, s).wait_send()
        for s in range(1, ns):
            second_copy(c, s).wait_send()
        for f in range(1, cols):
            square_copy(c, f).wait_send()


def update(cfg, dim, ids, total, squares, tables, accumulator, new_tables, new_acc,
           tab, acc, step, out_sem):
    ntab, width, per, group = cfg["ntab"], cfg["width"], cfg["per"], cfg["group"]
    pieces = cfg["pieces"]
    local_blocks = tables.shape[2] // BLOCK
    rows = 8
    parts = width // rows
    me = lax.axis_index("rep")

    def window(ref, t, d):
        return ref.at[t, pl.ds(d * rows, rows)]

    def store(t, d):
        return pltpu.make_async_copy(window(tab, t, d), window(new_tables, t, d), out_sem.at[t, d])

    def target(t, i):
        block = ids[t, me * per + i] - me * local_blocks
        return pl.ds(pl.multiple_of(block * BLOCK, BLOCK), BLOCK)

    new_acc[...] = accumulator[...]
    for t in range(ntab):
        for g in range(pieces):
            c = t * pieces + g
            for i in range(group):
                acc[c, pl.ds(i, 1), :] = accumulator[pl.ds(t, 1), target(t, g * group + i)]
            fresh = acc[c] + squares[c] * (1.0 / dim)
            acc[c] = fresh
            step[c] = 0.1 / (jnp.sqrt(fresh) + 1e-8)
            for i in range(group):
                new_acc[pl.ds(t, 1), target(t, g * group + i)] = acc[c, pl.ds(i, 1), :]
    for t in range(ntab):
        for d in range(parts):
            tab[t, pl.ds(d * rows, rows)] = tables[t, pl.ds(d * rows, rows)]
            for g in range(pieces):
                c = t * pieces + g
                for i in range(group):
                    where = target(t, g * group + i)
                    lanes = pl.ds(i * BLOCK, BLOCK)
                    moved = total[c, pl.ds(d * rows, rows), lanes] * step[c, pl.ds(i, 1), :]
                    tab[t, pl.ds(d * rows, rows), where] = tables[t, pl.ds(d * rows, rows), where] - moved
            store(t, d).start()
    for t in range(ntab):
        for d in range(parts):
            store(t, d).wait()


def body(mesh, tables, accumulator, replica_grads, block_ids):
    cfg = layout(mesh, tables.shape, replica_grads.shape[3])
    ntab, width, per, group = cfg["ntab"], cfg["width"], cfg["per"], cfg["group"]
    cols, pieces = cfg["cols"], cfg["pieces"]
    side = max(cfg["inner"], cfg["outer"])
    chunks, span = ntab * pieces, group * BLOCK
    dim = width * cols
    nslab = replica_grads.shape[3]
    nblk = nslab // BLOCK

    anyspace = pl.BlockSpec(memory_space=pl.ANY)
    vmem = pl.BlockSpec(memory_space=pltpu.VMEM)
    smem = pl.BlockSpec(memory_space=pltpu.SMEM)
    f32 = jnp.float32
    dma = pltpu.SemaphoreType.DMA
    packed, ids = pl.pallas_call(
        functools.partial(pack, cfg),
        out_shape=(jax.ShapeDtypeStruct((chunks, cfg["reps"], width, span), f32),
                   jax.ShapeDtypeStruct(block_ids.shape, jnp.int32)),
        in_specs=[vmem, vmem],
        out_specs=(vmem, vmem),
        scratch_shapes=[
            pltpu.VMEM((ntab, nblk), jnp.int32),
            pltpu.SMEM((ntab, nblk), jnp.int32),
            dma(()),
        ],
        compiler_params=pltpu.CompilerParams(vmem_limit_bytes=16 * 2**20),
        name="pack",
    )(block_ids, replica_grads)
    total, squares = pl.pallas_call(
        functools.partial(exchange, cfg),
        out_shape=(jax.ShapeDtypeStruct((chunks, width, span), f32),
                   jax.ShapeDtypeStruct((chunks, group, BLOCK), f32)),
        in_specs=[vmem],
        out_specs=(vmem, vmem),
        scratch_shapes=[
            pltpu.VMEM((chunks, side - 1, side, width, span), f32),
            pltpu.VMEM((chunks, side - 1, width, span), f32),
            pltpu.VMEM((chunks, side - 1, width, span), f32),
            pltpu.VMEM((chunks, cols, group, BLOCK), f32),
            dma((chunks, side - 1, side)), dma((chunks, side - 1, side)),
            dma((chunks, side - 1)), dma((chunks, side - 1)),
            dma((chunks, cols - 1)), dma((chunks, cols - 1)),
        ],
        compiler_params=pltpu.CompilerParams(
            collective_id=0, has_side_effects=True, vmem_limit_bytes=24 * 2**20),
        name="exchange",
    )(packed)
    rows = 8
    parts = width // rows
    return pl.pallas_call(
        functools.partial(update, cfg, dim),
        out_shape=(jax.ShapeDtypeStruct(tables.shape, f32),
                   jax.ShapeDtypeStruct(accumulator.shape, f32)),
        in_specs=[smem, vmem, vmem, vmem, vmem],
        out_specs=(anyspace, vmem),
        scratch_shapes=[
            pltpu.VMEM(tables.shape, f32),
            pltpu.VMEM((chunks, group, BLOCK), f32),
            pltpu.VMEM((chunks, group, BLOCK), f32),
            dma((ntab, parts)),
        ],
        compiler_params=pltpu.CompilerParams(vmem_limit_bytes=24 * 2**20),
        name="update",
    )(ids, total, squares, tables, accumulator)


def solution(mesh):
    return jax.shard_map(
        functools.partial(body, mesh),
        mesh=mesh,
        in_specs=(P(None, "col", "rep"), P(None, "rep"), P("rep", None, "col", None), P()),
        out_specs=(P(None, "col", "rep"), P(None, "rep")),
        check_vma=False,
    )
```

profile of v0, /device:TPU:0, one launch (start us, length us, event | category | flops | bytes accessed | tf_op | source)
XLA Modules:
  0.0 52.6 jit_solution(746325786938613238)
XLA Ops:
  0.6 0.0 copy-start.1
  0.6 1.6 %copy-done.1 = bf16[1,2,32,16384]{3,2,1,0:T(8,128)(2,1)S(1)} copy-done((bf16[1,2,32,16384]{3,2,1,0:T(8,128)(2,1)S(1)}, bf16[1,2,32,16384]{3,2,1,0:T(8,128)(2,1)}, u32[]{:S(2)}) %copy-start.1) | copy-done | bytes 2097176
  2.2 0.0 copy-start.3
  2.2 0.7 %copy-done.3 = s32[2,128]{1,0:T(2,128)S(1)} copy-done((s32[2,128]{1,0:T(2,128)S(1)}, s32[2,128]{1,0:T(2,128)}, u32[]{:S(2)}) %copy-start.3) | copy-done | bytes 1048
  2.9 1.4 %pack.1 = (f32[4,4,32,2048]{3,2,1,0:T(8,128)S(1)}, s32[2,128]{1,0:T(2,128)S(1)}) custom-call(s32[2,128]{1,0:T(2,128)S(1)} %copy-done.3, bf16[1,2,32,16384]{3,2,1,0:T(8,128)(2,1)S(1)} %copy-done.1), custom_call_target="tpu_custom_call" | custom-call | tf_op jit(solution)/shard_map/pack/pallas_call | solution.py:257
  4.3 0.0 copy-start
  4.3 0.0 copy-start.2
  4.4 45.3 %exchange.1 = (f32[4,32,2048]{2,1,0:T(8,128)S(1)}, f32[4,16,128]{2,1,0:T(8,128)S(1)}) custom-call(f32[4,4,32,2048]{3,2,1,0:T(8,128)S(1)} %get-tuple-element.7.packed), custom_call_target="tpu_custom_call" | custom-call | tf_op jit(solution)/shard_map/exchange/pallas_call | solution.py:271
  49.7 0.0 copy-done
  49.7 0.0 copy-done.2
  49.7 2.9 %update.1 = (f32[2,32,8192]{2,1,0:T(8,128)}, f32[2,8192]{1,0:T(2,128)}) custom-call(s32[2,128]{1,0:T(2,128)S(1)} %get-tuple-element.6.ids, f32[4,32,2048]{2,1,0:T(8,128)S(1)} %get-tuple-element.8.total, f32[4,16,128]{2,1,0:T(8,128)S(1)} %get-tuple-element.9.squares, f32[2,32,8192]{2,1,0:T(8,128)S(1)} %copy-done, f32[2,8192]{1,0:T(2,128)S(1)} %copy-done.2), custom_call_target="tpu_custom_call" | custom-call | tf_op jit(solution)/shard_map/update/pallas_call | solution.py:292
Async XLA Ops:
  0.6 1.6 %copy-start.1 = (bf16[1,2,32,16384]{3,2,1,0:T(8,128)(2,1)S(1)}, bf16[1,2,32,16384]{3,2,1,0:T(8,128)(2,1)}, u32[]{:S(2)}) copy-start(bf16[1,2,32,16384]{3,2,1,0:T(8,128)(2,1)} %grads.1) | copy-start | bytes 6291460
  2.2 0.7 %copy-start.3 = (s32[2,128]{1,0:T(2,128)S(1)}, s32[2,128]{1,0:T(2,128)}, u32[]{:S(2)}) copy-start(s32[2,128]{1,0:T(2,128)} %block_ids.1) | copy-start | bytes 3076
  4.3 45.3 %copy-start = (f32[2,32,8192]{2,1,0:T(8,128)S(1)}, f32[2,32,8192]{2,1,0:T(8,128)}, u32[]{:S(2)}) copy-start(f32[2,32,8192]{2,1,0:T(8,128)} %tables.1) | copy-start | bytes 6291460
  4.3 45.3 %copy-start.2 = (f32[2,8192]{1,0:T(2,128)S(1)}, f32[2,8192]{1,0:T(2,128)}, u32[]{:S(2)}) copy-start(f32[2,8192]{1,0:T(2,128)} %accumulator.1) | copy-start | bytes 196612
where the time goes:
time: 52.8 us; the launch traced here: 52.6 us
  Pallas kernels  49.7 us (94%)
  local copies, waits for them, and re-layouts  2.28 us (4%)
  between operations  0.69 us (1%)
    pallas_call x1, Pallas kernels, body(): pl.pallas_call(functools.partial(exchange, cfg), out_shape=(jax.ShapeDtyp...  45.3 us
    pallas_call x1, Pallas kernels, body(): pl.pallas_call(functools.partial(update, cfg, dim), out_shape=(jax.ShapeD...  2.93 us
    unnamed x8, local copies, waits for them, and re-layouts  2.28 us
    pallas_call x1, Pallas kernels, body(): pl.pallas_call(functools.partial(pack, cfg), out_shape=(jax.ShapeDtypeStr...  1.42 us

commit v1 on v0

v1 whole, which is shorter than its diff:
```python
import functools
import math

import jax
import jax.numpy as jnp
from jax import lax
from jax.experimental import pallas as pl
from jax.experimental.pallas import tpu as pltpu
from jax.sharding import PartitionSpec as P

BLOCK = 128
MESH = pl.DeviceIdType.MESH


def cuts(per, last):
    if per % 8:
        return [1] * per
    unit = per // 8
    return [2 * unit] * 2 + [unit] * 4 if last else [2 * unit] * 4


def layout(mesh, shape, n_slab):
    reps, cols = mesh.shape["rep"], mesh.shape["col"]
    inner = math.isqrt(reps)
    while reps % inner:
        inner -= 1
    ntab, width, local_rows = shape
    per = n_slab // BLOCK // reps
    pieces = []
    for t in range(ntab):
        start = 0
        for n in cuts(per, t == ntab - 1):
            pieces.append((t, start, n))
            start += n
    return dict(reps=reps, cols=cols, inner=inner, outer=reps // inner, ntab=ntab, width=width,
                per=per, nblk=n_slab // BLOCK, local=local_rows // BLOCK, dim=width * cols, pieces=pieces)


def lanes(i):
    return pl.ds(i * BLOCK, BLOCK)


def step_kernel(cfg, ids_hbm, grads_hbm, tables_hbm, acc_hbm, image, new_acc, *scratch):
    reps, cols, inner, outer = cfg["reps"], cfg["cols"], cfg["inner"], cfg["outer"]
    ntab, width, per, nblk = cfg["ntab"], cfg["width"], cfg["per"], cfg["nblk"]
    local, dim, pieces = cfg["local"], cfg["dim"], cfg["pieces"]
    n_pieces = len(pieces)
    scratch = list(scratch)

    def take(n):
        out = scratch[:n]
        del scratch[:n]
        return out

    g, totals = take(ntab), take(ntab)
    sq = take(n_pieces)
    (ids_v, order_v, code_v, order_s, code_s, packed, landed, relayed, landed2, acc_slot, step,
     in_sem, meta_sem, s1, r1, s2, r2, s3, r3) = scratch

    me = lax.axis_index("rep")
    my_col = lax.axis_index("col")
    x, y = lax.rem(me, inner), me // inner

    ids_copy = pltpu.make_async_copy(ids_hbm, ids_v, in_sem.at[0])
    ids_copy.start()
    grad_copies = [pltpu.make_async_copy(grads_hbm.at[0, t], g[t], in_sem.at[3 + t]) for t in range(ntab)]
    for copy in grad_copies:
        copy.start()

    barrier = pltpu.get_barrier_semaphore()
    for f in range(1, inner):
        pl.semaphore_signal(barrier, inc=1, device_id={"rep": y * inner + lax.rem(x + f, inner)}, device_id_type=MESH)
    for f in range(1, outer):
        pl.semaphore_signal(barrier, inc=1, device_id={"rep": lax.rem(y + f, outer) * inner + x}, device_id_type=MESH)
    for f in range(1, cols):
        pl.semaphore_signal(barrier, inc=1, device_id={"col": lax.rem(my_col + f, cols)}, device_id_type=MESH)

    acc_copy = pltpu.make_async_copy(acc_hbm, new_acc, in_sem.at[1])
    acc_copy.start()
    table_copy = pltpu.make_async_copy(tables_hbm, image, in_sem.at[2])
    table_copy.start()

    lane = lax.broadcasted_iota(jnp.int32, (nblk, nblk), 1)
    slot = lax.broadcasted_iota(jnp.int32, (nblk, nblk), 0)
    wide = code_v.shape[2]
    own_block = lax.broadcasted_iota(jnp.int32, (nblk, wide), 1) + me * local

    def order_copy(t):
        return pltpu.make_async_copy(order_v.at[t], order_s.at[t], meta_sem.at[0, t])

    def code_copy(t):
        return pltpu.make_async_copy(code_v.at[t], code_s.at[t], meta_sem.at[1, t])

    def rank_blocks(t):
        across = jnp.broadcast_to(ids_v[pl.ds(t, 1), :], (nblk, nblk))
        down = across.T
        place = jnp.sum(jnp.where(down < across, 1, 0), axis=0, keepdims=True)
        hit = jnp.broadcast_to(place, (nblk, nblk)).T == lane
        order = jnp.sum(jnp.where(hit, slot, 0), axis=0, keepdims=True)
        block = jnp.sum(jnp.where(hit, down, 0), axis=0, keepdims=True) - me * local
        order_v[t, pl.ds(0, 1), :] = jnp.clip(order, 0, nblk - 1)
        order_v[t, pl.ds(1, 1), :] = jnp.clip(block, 0, local - 1)
        order_copy(t).start()
        col = jnp.broadcast_to(down[:, :1], (nblk, wide))
        below = jnp.sum(jnp.where(col < own_block, 1, 0), axis=0, keepdims=True) - me * per
        found = jnp.sum(jnp.where(col == own_block, 1, 0), axis=0, keepdims=True)
        code_v[t, pl.ds(0, 1), :] = jnp.where(found > 0, jnp.clip(below, 0, per - 1), -1)
        code_copy(t).start()

    ids_copy.wait()
    for t in range(ntab):
        rank_blocks(t)

    def axes(p):
        return (inner, outer) if p % 2 == 0 else (outer, inner)

    def rank(p, f, s):
        if p % 2 == 0:
            return lax.rem(y + s, outer) * inner + lax.rem(x + f, inner)
        return lax.rem(y + f, outer) * inner + lax.rem(x + s, inner)

    def span(p):
        t, start, n = pieces[p]
        return pl.ds(t * per + start, n)

    def mine(t, owner, i):
        at = order_s[t, 0, owner * per + i]
        return g[t][:, lanes(at)].astype(jnp.float32)

    def first_copy(p, f, s):
        return pltpu.make_async_remote_copy(
            packed.at[f - 1, s, span(p)], landed.at[f - 1, s, span(p)], s1.at[p, f - 1, s], r1.at[p, f - 1, s],
            device_id={"rep": rank(p, f, 0)}, device_id_type=MESH)

    def second_copy(p, s):
        return pltpu.make_async_remote_copy(
            relayed.at[s - 1, span(p)], landed2.at[s - 1, span(p)], s2.at[p, s - 1], r2.at[p, s - 1],
            device_id={"rep": rank(p, 0, s)}, device_id_type=MESH)

    def square_copy(p, f):
        return pltpu.make_async_remote_copy(
            sq[p].at[my_col], sq[p].at[my_col], s3.at[p, f - 1], r3.at[p, f - 1],
            device_id={"col": lax.rem(my_col + f, cols)}, device_id_type=MESH)

    def pack(p, f, s):
        t, start, n = pieces[p]
        owner = rank(p, f, s)
        for i in range(n):
            packed[f - 1, s, t * per + start + i] = mine(t, owner, start + i)
        first_copy(p, f, s).start()

    def send_far(p):
        nf, ns = axes(p)
        for s in range(1, ns):
            for f in range(1, nf):
                pack(p, f, s)

    def send_near(p):
        for f in range(1, axes(p)[0]):
            pack(p, f, 0)

    def relay(p):
        t, start, n = pieces[p]
        nf, ns = axes(p)
        for s in range(1, ns):
            for f in range(1, nf):
                first_copy(p, f, s).wait_recv()
            owner = rank(p, 0, s)
            for i in range(n):
                acc = mine(t, owner, start + i)
                for f in range(1, nf):
                    acc = acc + landed[f - 1, s, t * per + start + i]
                relayed[s - 1, t * per + start + i] = acc
            second_copy(p, s).start()

    def finish(p):
        t, start, n = pieces[p]
        nf, ns = axes(p)
        for f in range(1, nf):
            first_copy(p, f, 0).wait_recv()
        for s in range(1, ns):
            second_copy(p, s).wait_recv()
        for i in range(n):
            acc = mine(t, me, start + i)
            for f in range(1, nf):
                acc = acc + landed[f - 1, 0, t * per + start + i]
            for s in range(1, ns):
                acc = acc + landed2[s - 1, t * per + start + i]
            totals[t][start + i] = acc
            sq[p][my_col, pl.ds(i, 1), :] = jnp.sum(acc * acc, axis=0, keepdims=True)
        for f in range(1, cols):
            square_copy(p, f).start()

    def gather(p):
        t, start, n = pieces[p]
        for f in range(1, cols):
            square_copy(p, f).wait_recv()
        acc = sq[p][0]
        for f in range(1, cols):
            acc = acc + sq[p][f]
        fresh = acc_slot[t, pl.ds(start, n), :] + acc * (1.0 / dim)
        acc_slot[t, pl.ds(start, n), :] = fresh
        step[t, pl.ds(start, n), :] = 0.1 / (jnp.sqrt(fresh) + 1e-8)
        for i in range(start, start + n):
            totals[t][i] = totals[t][i] * step[t, pl.ds(i, 1), :]

    def place(t):
        for b in range(local):
            code = code_s[t, 0, b]
            at = jnp.maximum(code, 0)
            where = pl.ds(b * BLOCK, BLOCK)
            hit = jnp.full((width, BLOCK), code, jnp.int32) >= 0
            old = image[t, :, where]
            image[t, :, where] = jnp.where(hit, old - totals[t][at], old)
            old_acc = new_acc[pl.ds(t, 1), where]
            new_acc[pl.ds(t, 1), where] = jnp.where(hit[:1], acc_slot[t, pl.ds(at, 1), :], old_acc)

    for t in range(ntab):
        order_copy(t).wait()
        grad_copies[t].wait()
        if t == 0:
            pl.semaphore_wait(barrier, inner - 1 + outer - 1 + cols - 1)
        for p in range(n_pieces):
            if pieces[p][0] == t:
                send_far(p)
    for p in range(n_pieces):
        send_near(p)

    acc_copy.wait()
    for t in range(ntab):
        for i in range(per):
            block = order_s[t, 1, me * per + i]
            acc_slot[t, pl.ds(i, 1), :] = new_acc[pl.ds(t, 1), lanes(block)]

    for p in range(n_pieces):
        relay(p)
    table_copy.wait()
    for t in range(ntab):
        code_copy(t).wait()
    for p in range(n_pieces + 1):
        if p < n_pieces:
            finish(p)
        if p > 0:
            gather(p - 1)
            t = pieces[p - 1][0]
            if p == n_pieces or pieces[p][0] != t:
                place(t)

    for p in range(n_pieces):
        nf, ns = axes(p)
        for s in range(ns):
            for f in range(1, nf):
                first_copy(p, f, s).wait_send()
        for s in range(1, ns):
            second_copy(p, s).wait_send()
        for f in range(1, cols):
            square_copy(p, f).wait_send()


def store_kernel(image, acc, tables_out, acc_out, sem, acc_sem):
    copies = [pltpu.make_async_copy(acc, acc_out, acc_sem)]
    for t in range(image.shape[0]):
        for d in range(image.shape[1] // 8):
            rows = pl.ds(d * 8, 8)
            copies.append(pltpu.make_async_copy(image.at[t, rows], tables_out.at[t, rows], sem.at[t, d]))
    for copy in copies:
        copy.start()
    for copy in copies:
        copy.wait()


def body(mesh, tables, accumulator, replica_grads, block_ids):
    cfg = layout(mesh, tables.shape, replica_grads.shape[3])
    ntab, width, per, nblk = cfg["ntab"], cfg["width"], cfg["per"], cfg["nblk"]
    cols, pieces = cfg["cols"], cfg["pieces"]
    side = max(cfg["inner"], cfg["outer"])
    slots, n_pieces = ntab * per, len(pieces)
    wide = -(-cfg["local"] // BLOCK) * BLOCK
    f32, i32 = jnp.float32, jnp.int32
    dma = pltpu.SemaphoreType.DMA
    hbm = pl.BlockSpec(memory_space=pltpu.HBM)
    vmem = pl.BlockSpec(memory_space=pltpu.VMEM)
    image, new_acc = pl.pallas_call(
        functools.partial(step_kernel, cfg),
        out_shape=(jax.ShapeDtypeStruct(tables.shape, f32), jax.ShapeDtypeStruct(accumulator.shape, f32)),
        in_specs=[hbm] * 4,
        out_specs=(vmem, vmem),
        scratch_shapes=[
            *[pltpu.VMEM(replica_grads.shape[2:], replica_grads.dtype) for _ in range(ntab)],
            *[pltpu.VMEM((per, width, BLOCK), f32) for _ in range(ntab)],
            *[pltpu.VMEM((cols, n, BLOCK), f32) for _, _, n in pieces],
            pltpu.VMEM(block_ids.shape, i32),
            pltpu.VMEM((ntab, 2, nblk), i32),
            pltpu.VMEM((ntab, 1, wide), i32),
            pltpu.SMEM((ntab, 2, nblk), i32),
            pltpu.SMEM((ntab, 1, wide), i32),
            pltpu.VMEM((side - 1, side, slots, width, BLOCK), f32),
            pltpu.VMEM((side - 1, side, slots, width, BLOCK), f32),
            pltpu.VMEM((side - 1, slots, width, BLOCK), f32),
            pltpu.VMEM((side - 1, slots, width, BLOCK), f32),
            pltpu.VMEM((ntab, per, BLOCK), f32),
            pltpu.VMEM((ntab, per, BLOCK), f32),
            dma((3 + ntab,)), dma((2, ntab)),
            dma((n_pieces, side - 1, side)), dma((n_pieces, side - 1, side)),
            dma((n_pieces, side - 1)), dma((n_pieces, side - 1)),
            dma((n_pieces, cols - 1)), dma((n_pieces, cols - 1)),
        ],
        compiler_params=pltpu.CompilerParams(
            collective_id=0, has_side_effects=True, vmem_limit_bytes=32 * 2**20),
        name="exchange",
    )(*[pltpu.with_memory_space_constraint(a, pltpu.HBM) for a in (block_ids, replica_grads, tables, accumulator)])
    return pl.pallas_call(
        store_kernel,
        out_shape=(jax.ShapeDtypeStruct(tables.shape, f32), jax.ShapeDtypeStruct(accumulator.shape, f32)),
        in_specs=[vmem, vmem],
        out_specs=(hbm, hbm),
        scratch_shapes=[dma((ntab, width // 8)), dma(())],
        compiler_params=pltpu.CompilerParams(vmem_limit_bytes=2**20),
        name="store",
    )(image, new_acc)


def solution(mesh):
    return jax.shard_map(
        functools.partial(body, mesh),
        mesh=mesh,
        in_specs=(P(None, "col", "rep"), P(None, "rep"), P("rep", None, "col", None), P()),
        out_specs=(P(None, "col", "rep"), P(None, "rep")),
        check_vma=False,
    )
```

time: 52.8 us -> 56 us (1.061)
  Pallas kernels: 49.7 us -> 55.2 us
  local copies, waits for them, and re-layouts: 2.28 us -> 0 us
    pallas_call x3 -> x2, Pallas kernels: 49.7 us -> 55.2 us  [the longest x1 53.7 us: body(): pl.pallas_call(functools.partial(step_kernel, cfg), out_shape=(jax.ShapeD...]
    unnamed x8 -> x0, local copies, waits for them, and re-layouts: 2.28 us -> none
where the time goes in v1:
time: 56 us; the launch traced here: 55.8 us
  Pallas kernels  55.2 us (99%)
  between operations  0.64 us (1%)
    pallas_call x1, Pallas kernels, body(): pl.pallas_call(functools.partial(step_kernel, cfg), out_shape=(jax.ShapeD...  53.7 us
    pallas_call x1, Pallas kernels, body(): pl.pallas_call(store_kernel, out_shape=(jax.ShapeDtypeStruct(tables.shape...  1.41 us

profile of v1, /device:TPU:0, one launch (start us, length us, event | category | flops | bytes accessed | tf_op | source)
XLA Modules:
  0.0 55.8 jit_solution(2580876928814811321)
XLA Ops:
  0.6 53.7 %exchange.1 = (f32[2,32,8192]{2,1,0:T(8,128)S(1)}, f32[2,8192]{1,0:T(2,128)S(1)}) custom-call(s32[2,128]{1,0:T(2,128)} %ids_hbm.1, bf16[1,2,32,16384]{3,2,1,0:T(8,128)(2,1)} %grads_hbm.1, f32[2,32,8192]{2,1,0:T(8,128)} %tables_hbm.1, f32[2,8192]{1,0:T(2,128)} %acc_hbm.1), custom_call_target="tpu_custom_call" | custom-call | tf_op jit(solution)/shard_map/exchange/pallas_call | solution.py:283
  54.4 1.4 %store.1 = (f32[2,32,8192]{2,1,0:T(8,128)}, f32[2,8192]{1,0:T(2,128)}) custom-call(f32[2,32,8192]{2,1,0:T(8,128)S(1)} %get-tuple-element.4.image, f32[2,8192]{1,0:T(2,128)S(1)} %get-tuple-element.5.acc), custom_call_target="tpu_custom_call" | custom-call | tf_op jit(solution)/shard_map/store/pallas_call | solution.py:312

commit v2 on v1

--- a/solution.py
+++ b/solution.py
@@ -108,8 +108,7 @@
         code_copy(t).start()
 
     ids_copy.wait()
-    for t in range(ntab):
-        rank_blocks(t)
+    rank_blocks(0)
 
     def axes(p):
         return (inner, outer) if p % 2 == 0 else (outer, inner)
@@ -223,6 +222,8 @@
         for p in range(n_pieces):
             if pieces[p][0] == t:
                 send_far(p)
+        if t + 1 < ntab:
+            rank_blocks(t + 1)
     for p in range(n_pieces):
         send_near(p)
 
@@ -237,14 +238,13 @@
     table_copy.wait()
     for t in range(ntab):
         code_copy(t).wait()
-    for p in range(n_pieces + 1):
-        if p < n_pieces:
-            finish(p)
-        if p > 0:
-            gather(p - 1)
-            t = pieces[p - 1][0]
-            if p == n_pieces or pieces[p][0] != t:
-                place(t)
+    for p in range(n_pieces):
+        finish(p)
+    for p in range(n_pieces):
+        gather(p)
+        t = pieces[p][0]
+        if p + 1 == n_pieces or pieces[p + 1][0] != t:
+            place(t)
 
     for p in range(n_pieces):
         nf, ns = axes(p)

time: 56 us -> 48.7 us (0.87)
  Pallas kernels: 55.2 us -> 47.8 us
    pallas_call x1, Pallas kernels: 53.7 us -> 46.4 us  [body(): pl.pallas_call(functools.partial(step_kernel, cfg), out_shape=(jax.ShapeD...]
where the time goes in v2:
time: 48.7 us; the launch traced here: 48.5 us
  Pallas kernels  47.8 us (98%)
  between operations  0.64 us (1%)
    pallas_call x1, Pallas kernels, body(): pl.pallas_call(functools.partial(step_kernel, cfg), out_shape=(jax.ShapeD...  46.4 us
    pallas_call x1, Pallas kernels, body(): pl.pallas_call(store_kernel, out_shape=(jax.ShapeDtypeStruct(tables.shape...  1.41 us

profile of v2, /device:TPU:0, one launch (start us, length us, event | category | flops | bytes accessed | tf_op | source)
XLA Modules:
  0.0 48.5 jit_solution(16342238288071201778)
XLA Ops:
  0.6 46.4 %exchange.1 = (f32[2,32,8192]{2,1,0:T(8,128)S(1)}, f32[2,8192]{1,0:T(2,128)S(1)}) custom-call(s32[2,128]{1,0:T(2,128)} %ids_hbm.1, bf16[1,2,32,16384]{3,2,1,0:T(8,128)(2,1)} %grads_hbm.1, f32[2,32,8192]{2,1,0:T(8,128)} %tables_hbm.1, f32[2,8192]{1,0:T(2,128)} %acc_hbm.1), custom_call_target="tpu_custom_call" | custom-call | tf_op jit(solution)/shard_map/exchange/pallas_call | solution.py:283
  47.1 1.4 %store.1 = (f32[2,32,8192]{2,1,0:T(8,128)}, f32[2,8192]{1,0:T(2,128)}) custom-call(f32[2,32,8192]{2,1,0:T(8,128)S(1)} %get-tuple-element.4.image, f32[2,8192]{1,0:T(2,128)S(1)} %get-tuple-element.5.acc), custom_call_target="tpu_custom_call" | custom-call | tf_op jit(solution)/shard_map/store/pallas_call | solution.py:312

commit v3 on v2

--- a/solution.py
+++ b/solution.py
@@ -54,8 +54,8 @@
 
     g, totals = take(ntab), take(ntab)
     sq = take(n_pieces)
-    (ids_v, order_v, code_v, order_s, code_s, packed, landed, relayed, landed2, acc_slot, step,
-     in_sem, meta_sem, s1, r1, s2, r2, s3, r3) = scratch
+    (ids_v, order_v, code_v, order_s, code_s, packed, landed, relayed, arrived, acc_slot, step, sent,
+     in_sem, meta_sem, send_sem, far_sem, own_sem, sq_sem, up, down) = scratch
 
     me = lax.axis_index("rep")
     my_col = lax.axis_index("col")
@@ -72,8 +72,12 @@
         pl.semaphore_signal(barrier, inc=1, device_id={"rep": y * inner + lax.rem(x + f, inner)}, device_id_type=MESH)
     for f in range(1, outer):
         pl.semaphore_signal(barrier, inc=1, device_id={"rep": lax.rem(y + f, outer) * inner + x}, device_id_type=MESH)
-    for f in range(1, cols):
-        pl.semaphore_signal(barrier, inc=1, device_id={"col": lax.rem(my_col + f, cols)}, device_id_type=MESH)
+
+    def pass_on(sem, way):
+        pl.semaphore_signal(sem, inc=1, device_id={"col": my_col + way}, device_id_type=MESH)
+
+    pl.when(my_col > 0)(lambda: pass_on(barrier, -1))
+    pl.when(my_col < cols - 1)(lambda: pass_on(barrier, 1))
 
     acc_copy = pltpu.make_async_copy(acc_hbm, new_acc, in_sem.at[1])
     acc_copy.start()
@@ -127,19 +131,24 @@
         return g[t][:, lanes(at)].astype(jnp.float32)
 
     def first_copy(p, f, s):
+        here = arrived.at[f - 1, span(p)] if s == 0 else landed.at[f - 1, s - 1, span(p)]
         return pltpu.make_async_remote_copy(
-            packed.at[f - 1, s, span(p)], landed.at[f - 1, s, span(p)], s1.at[p, f - 1, s], r1.at[p, f - 1, s],
+            packed.at[f - 1, s, span(p)], here, send_sem.at[0], own_sem.at[p] if s == 0 else far_sem.at[p],
             device_id={"rep": rank(p, f, 0)}, device_id_type=MESH)
 
     def second_copy(p, s):
+        nf = axes(p)[0]
         return pltpu.make_async_remote_copy(
-            relayed.at[s - 1, span(p)], landed2.at[s - 1, span(p)], s2.at[p, s - 1], r2.at[p, s - 1],
+            relayed.at[s - 1, span(p)], arrived.at[nf - 2 + s, span(p)], send_sem.at[1], own_sem.at[p],
             device_id={"rep": rank(p, 0, s)}, device_id_type=MESH)
 
     def square_copy(p, f):
         return pltpu.make_async_remote_copy(
-            sq[p].at[my_col], sq[p].at[my_col], s3.at[p, f - 1], r3.at[p, f - 1],
+            sq[p].at[my_col], sq[p].at[my_col], send_sem.at[2], sq_sem.at[p],
             device_id={"col": lax.rem(my_col + f, cols)}, device_id_type=MESH)
+
+    def wait_all(ref, sem):
+        pltpu.make_async_copy(ref, ref, sem).wait()
 
     def pack(p, f, s):
         t, start, n = pieces[p]
@@ -161,30 +170,24 @@
     def relay(p):
         t, start, n = pieces[p]
         nf, ns = axes(p)
+        wait_all(landed.at[pl.ds(0, nf - 1), pl.ds(0, ns - 1), span(p)], far_sem.at[p])
         for s in range(1, ns):
-            for f in range(1, nf):
-                first_copy(p, f, s).wait_recv()
             owner = rank(p, 0, s)
             for i in range(n):
                 acc = mine(t, owner, start + i)
                 for f in range(1, nf):
-                    acc = acc + landed[f - 1, s, t * per + start + i]
+                    acc = acc + landed[f - 1, s - 1, t * per + start + i]
                 relayed[s - 1, t * per + start + i] = acc
             second_copy(p, s).start()
 
     def finish(p):
         t, start, n = pieces[p]
         nf, ns = axes(p)
-        for f in range(1, nf):
-            first_copy(p, f, 0).wait_recv()
-        for s in range(1, ns):
-            second_copy(p, s).wait_recv()
+        wait_all(arrived.at[pl.ds(0, nf + ns - 2), span(p)], own_sem.at[p])
         for i in range(n):
             acc = mine(t, me, start + i)
-            for f in range(1, nf):
-                acc = acc + landed[f - 1, 0, t * per + start + i]
-            for s in range(1, ns):
-                acc = acc + landed2[s - 1, t * per + start + i]
+            for k in range(nf + ns - 2):
+                acc = acc + arrived[k, t * per + start + i]
             totals[t][start + i] = acc
             sq[p][my_col, pl.ds(i, 1), :] = jnp.sum(acc * acc, axis=0, keepdims=True)
         for f in range(1, cols):
@@ -192,8 +195,7 @@
 
     def gather(p):
         t, start, n = pieces[p]
-        for f in range(1, cols):
-            square_copy(p, f).wait_recv()
+        wait_all(sq[p].at[pl.ds(0, cols - 1)], sq_sem.at[p])
         acc = sq[p][0]
         for f in range(1, cols):
             acc = acc + sq[p][f]
@@ -214,11 +216,16 @@
             old_acc = new_acc[pl.ds(t, 1), where]
             new_acc[pl.ds(t, 1), where] = jnp.where(hit[:1], acc_slot[t, pl.ds(at, 1), :], old_acc)
 
+    def sweep(sem, way, behind, ahead):
+        pl.when(behind)(lambda: pl.semaphore_wait(sem, 1))
+        pl.when(ahead)(lambda: pass_on(sem, way))
+
     for t in range(ntab):
         order_copy(t).wait()
         grad_copies[t].wait()
         if t == 0:
-            pl.semaphore_wait(barrier, inner - 1 + outer - 1 + cols - 1)
+            beside = jnp.minimum(my_col, 1) + jnp.minimum(cols - 1 - my_col, 1)
+            pl.semaphore_wait(barrier, inner - 1 + outer - 1 + beside)
         for p in range(n_pieces):
             if pieces[p][0] == t:
                 send_far(p)
@@ -235,6 +242,8 @@
 
     for p in range(n_pieces):
         relay(p)
+    sweep(up, 1, my_col > 0, my_col < cols - 1)
+    sweep(down, -1, my_col < cols - 1, my_col > 0)
     table_copy.wait()
     for t in range(ntab):
         code_copy(t).wait()
@@ -246,15 +255,15 @@
         if p + 1 == n_pieces or pieces[p + 1][0] != t:
             place(t)
 
-    for p in range(n_pieces):
-        nf, ns = axes(p)
-        for s in range(ns):
-            for f in range(1, nf):
-                first_copy(p, f, s).wait_send()
-        for s in range(1, ns):
-            second_copy(p, s).wait_send()
-        for f in range(1, cols):
-            square_copy(p, f).wait_send()
+    if inner == outer:
+        wait_all(packed, send_sem.at[0])
+        wait_all(relayed, send_sem.at[1])
+    else:
+        for p in range(n_pieces):
+            nf, ns = axes(p)
+            wait_all(packed.at[pl.ds(0, nf - 1), pl.ds(0, ns), span(p)], send_sem.at[0])
+            wait_all(relayed.at[pl.ds(0, ns - 1), span(p)], send_sem.at[1])
+    wait_all(sent, send_sem.at[2])
 
 
 def store_kernel(image, acc, tables_out, acc_out, sem, acc_sem):
@@ -295,15 +304,15 @@
             pltpu.SMEM((ntab, 2, nblk), i32),
             pltpu.SMEM((ntab, 1, wide), i32),
             pltpu.VMEM((side - 1, side, slots, width, BLOCK), f32),
-            pltpu.VMEM((side - 1, side, slots, width, BLOCK), f32),
+            pltpu.VMEM((side - 1, side - 1, slots, width, BLOCK), f32),
             pltpu.VMEM((side - 1, slots, width, BLOCK), f32),
-            pltpu.VMEM((side - 1, slots, width, BLOCK), f32),
+            pltpu.VMEM((2 * side - 2, slots, width, BLOCK), f32),
             pltpu.VMEM((ntab, per, BLOCK), f32),
             pltpu.VMEM((ntab, per, BLOCK), f32),
-            dma((3 + ntab,)), dma((2, ntab)),
-            dma((n_pieces, side - 1, side)), dma((n_pieces, side - 1, side)),
-            dma((n_pieces, side - 1)), dma((n_pieces, side - 1)),
-            dma((n_pieces, cols - 1)), dma((n_pieces, cols - 1)),
+            pltpu.VMEM((cols - 1, slots, BLOCK), f32),
+            dma((3 + ntab,)), dma((2, ntab)), dma((3,)),
+            dma((n_pieces,)), dma((n_pieces,)), dma((n_pieces,)),
+            pltpu.SemaphoreType.REGULAR, pltpu.SemaphoreType.REGULAR,
         ],
         compiler_params=pltpu.CompilerParams(
             collective_id=0, has_side_effects=True, vmem_limit_bytes=32 * 2**20),

time: 48.7 us -> 47 us (0.965)
  Pallas kernels: 47.8 us -> 46.2 us
    pallas_call x1, Pallas kernels: 46.4 us -> 44.8 us  [body(): pl.pallas_call(functools.partial(step_kernel, cfg), out_shape=(jax.ShapeD...]
where the time goes in v3:
time: 47 us; the launch traced here: 46.9 us
  Pallas kernels  46.2 us (98%)
  between operations  0.64 us (1%)
    pallas_call x1, Pallas kernels, body(): pl.pallas_call(functools.partial(step_kernel, cfg), out_shape=(jax.ShapeD...  44.8 us
    pallas_call x1, Pallas kernels, body(): pl.pallas_call(store_kernel, out_shape=(jax.ShapeDtypeStruct(tables.shape...  1.41 us

profile of v3, /device:TPU:0, one launch (start us, length us, event | category | flops | bytes accessed | tf_op | source)
XLA Modules:
  0.0 46.9 jit_solution(11479607358819119298)
XLA Ops:
  0.6 44.8 %exchange.1 = (f32[2,32,8192]{2,1,0:T(8,128)S(1)}, f32[2,8192]{1,0:T(2,128)S(1)}) custom-call(s32[2,128]{1,0:T(2,128)} %ids_hbm.1, bf16[1,2,32,16384]{3,2,1,0:T(8,128)(2,1)} %grads_hbm.1, f32[2,32,8192]{2,1,0:T(8,128)} %tables_hbm.1, f32[2,8192]{1,0:T(2,128)} %acc_hbm.1), custom_call_target="tpu_custom_call" | custom-call | tf_op jit(solution)/shard_map/exchange/pallas_call | solution.py:292
  45.4 1.4 %store.1 = (f32[2,32,8192]{2,1,0:T(8,128)}, f32[2,8192]{1,0:T(2,128)}) custom-call(f32[2,32,8192]{2,1,0:T(8,128)S(1)} %get-tuple-element.4.image, f32[2,8192]{1,0:T(2,128)S(1)} %get-tuple-element.5.acc), custom_call_target="tpu_custom_call" | custom-call | tf_op jit(solution)/shard_map/store/pallas_call | solution.py:321

commit v4 on v3

--- a/solution.py
+++ b/solution.py
@@ -16,7 +16,8 @@
     if per % 8:
         return [1] * per
     unit = per // 8
-    return [2 * unit] * 2 + [unit] * 4 if last else [2 * unit] * 4
+    tail = max(1, 3 * unit // 4)
+    return [2 * unit] * 2 + [2 * unit - tail] * 2 + [tail] * 2 if last else [4 * unit] * 2
 
 
 def layout(mesh, shape, n_slab):
@@ -32,7 +33,8 @@
         for n in cuts(per, t == ntab - 1):
             pieces.append((t, start, n))
             start += n
-    return dict(reps=reps, cols=cols, inner=inner, outer=reps // inner, ntab=ntab, width=width,
+    steered = 2 if inner == 2 and reps == 4 else 0
+    return dict(steered=steered, reps=reps, cols=cols, inner=inner, outer=reps // inner, ntab=ntab, width=width,
                 per=per, nblk=n_slab // BLOCK, local=local_rows // BLOCK, dim=width * cols, pieces=pieces)
 
 
@@ -54,8 +56,9 @@
 
     g, totals = take(ntab), take(ntab)
     sq = take(n_pieces)
-    (ids_v, order_v, code_v, order_s, code_s, packed, landed, relayed, arrived, acc_slot, step, sent,
-     in_sem, meta_sem, send_sem, far_sem, own_sem, sq_sem, up, down) = scratch
+    (ids_v, order_v, code_v, order_s, code_s, packed, landed, relayed, arrived, acc_slot, step, sent, spare,
+     in_sem, meta_sem, send_sem, far_sem, own_sem, sq_sem, up, down, spare_sem) = scratch
+    first_steered = n_pieces - cfg["steered"]
 
     me = lax.axis_index("rep")
     my_col = lax.axis_index("col")
@@ -157,17 +160,63 @@
             packed[f - 1, s, t * per + start + i] = mine(t, owner, start + i)
         first_copy(p, f, s).start()
 
+    beside_me = (y * inner + lax.rem(x + 1, inner), lax.rem(y + 1, outer) * inner + x)
+    across_me = lax.rem(y + 1, outer) * inner + lax.rem(x + 1, inner)
+
+    def way(p, owner):
+        return jnp.where(owner == 1, 0, jnp.where(owner == inner, 1, p % 2))
+
+    def steered_far(p):
+        t, start, n = pieces[p]
+        first = way(p, across_me)
+        for i in range(n):
+            packed[0, 1, t * per + start + i] = mine(t, across_me, start + i)
+        b = p - first_steered
+        pltpu.make_async_remote_copy(
+            packed.at[0, 1, span(p)], spare.at[first, b], send_sem.at[0], spare_sem.at[first, b],
+            device_id={"rep": jnp.where(first == 0, beside_me[0], beside_me[1])}, device_id_type=MESH).start()
+
+    def steered_send(p, d, relaying):
+        t, start, n = pieces[p]
+        owner, b = beside_me[d], p - first_steered
+        out = packed.at[0, 0] if d == 0 else relayed.at[0]
+
+        def send():
+            if relaying:
+                wait_all(spare.at[1 - d, b], spare_sem.at[1 - d, b])
+            for i in range(n):
+                acc = mine(t, owner, start + i)
+                if relaying:
+                    acc = acc + spare[1 - d, b, i]
+                out[t * per + start + i] = acc
+            pltpu.make_async_remote_copy(
+                out.at[span(p)], arrived.at[d, span(p)], send_sem.at[d], own_sem.at[p],
+                device_id={"rep": owner}, device_id_type=MESH).start()
+
+        pl.when((way(p, owner) != d) if relaying else (way(p, owner) == d))(send)
+
     def send_far(p):
+        if p >= first_steered:
+            steered_far(p)
+            return
         nf, ns = axes(p)
         for s in range(1, ns):
             for f in range(1, nf):
                 pack(p, f, s)
 
     def send_near(p):
+        if p >= first_steered:
+            for d in range(2):
+                steered_send(p, d, False)
+            return
         for f in range(1, axes(p)[0]):
             pack(p, f, 0)
 
     def relay(p):
+        if p >= first_steered:
+            for d in range(2):
+                steered_send(p, d, True)
+            return
         t, start, n = pieces[p]
         nf, ns = axes(p)
         wait_all(landed.at[pl.ds(0, nf - 1), pl.ds(0, ns - 1), span(p)], far_sem.at[p])
@@ -269,9 +318,7 @@
 def store_kernel(image, acc, tables_out, acc_out, sem, acc_sem):
     copies = [pltpu.make_async_copy(acc, acc_out, acc_sem)]
     for t in range(image.shape[0]):
-        for d in range(image.shape[1] // 8):
-            rows = pl.ds(d * 8, 8)
-            copies.append(pltpu.make_async_copy(image.at[t, rows], tables_out.at[t, rows], sem.at[t, d]))
+        copies.append(pltpu.make_async_copy(image.at[t], tables_out.at[t], sem.at[t]))
     for copy in copies:
         copy.start()
     for copy in copies:
@@ -310,9 +357,10 @@
             pltpu.VMEM((ntab, per, BLOCK), f32),
             pltpu.VMEM((ntab, per, BLOCK), f32),
             pltpu.VMEM((cols - 1, slots, BLOCK), f32),
+            pltpu.VMEM((2, 2, pieces[-1][2], width, BLOCK), f32),
             dma((3 + ntab,)), dma((2, ntab)), dma((3,)),
             dma((n_pieces,)), dma((n_pieces,)), dma((n_pieces,)),
-            pltpu.SemaphoreType.REGULAR, pltpu.SemaphoreType.REGULAR,
+            pltpu.SemaphoreType.REGULAR, pltpu.SemaphoreType.REGULAR, dma((2, 2)),
         ],
         compiler_params=pltpu.CompilerParams(
             collective_id=0, has_side_effects=True, vmem_limit_bytes=32 * 2**20),
@@ -323,7 +371,7 @@
         out_shape=(jax.ShapeDtypeStruct(tables.shape, f32), jax.ShapeDtypeStruct(accumulator.shape, f32)),
         in_specs=[vmem, vmem],
         out_specs=(hbm, hbm),
-        scratch_shapes=[dma((ntab, width // 8)), dma(())],
+        scratch_shapes=[dma((ntab,)), dma(())],
         compiler_params=pltpu.CompilerParams(vmem_limit_bytes=2**20),
         name="store",
     )(image, new_acc)

time: 47 us -> 45.9 us (0.977)
  Pallas kernels: 46.2 us -> 45.1 us
    pallas_call x1, Pallas kernels: 44.8 us -> 43.7 us  [body(): pl.pallas_call(functools.partial(step_kernel, cfg), out_shape=(jax.ShapeD...]
where the time goes in v4:
time: 45.9 us; the launch traced here: 45.7 us
  Pallas kernels  45.1 us (98%)
  between operations  0.64 us (1%)
    pallas_call x1, Pallas kernels, body(): pl.pallas_call(functools.partial(step_kernel, cfg), out_shape=(jax.ShapeD...  43.7 us
    pallas_call x1, Pallas kernels, body(): pl.pallas_call(store_kernel, out_shape=(jax.ShapeDtypeStruct(tables.shape...  1.37 us

profile of v4, /device:TPU:0, one launch (start us, length us, event | category | flops | bytes accessed | tf_op | source)
XLA Modules:
  0.0 45.7 jit_solution(12100813021498971507)
XLA Ops:
  0.6 43.7 %exchange.1 = (f32[2,32,8192]{2,1,0:T(8,128)S(1)}, f32[2,8192]{1,0:T(2,128)S(1)}) custom-call(s32[2,128]{1,0:T(2,128)} %ids_hbm.1, bf16[1,2,32,16384]{3,2,1,0:T(8,128)(2,1)} %grads_hbm.1, f32[2,32,8192]{2,1,0:T(8,128)} %tables_hbm.1, f32[2,8192]{1,0:T(2,128)} %acc_hbm.1), custom_call_target="tpu_custom_call" | custom-call | tf_op jit(solution)/shard_map/exchange/pallas_call | solution.py:339
  44.4 1.4 %store.1 = (f32[2,32,8192]{2,1,0:T(8,128)}, f32[2,8192]{1,0:T(2,128)}) custom-call(f32[2,32,8192]{2,1,0:T(8,128)S(1)} %get-tuple-element.4.image, f32[2,8192]{1,0:T(2,128)S(1)} %get-tuple-element.5.acc), custom_call_target="tpu_custom_call" | custom-call | tf_op jit(solution)/shard_map/store/pallas_call | solution.py:369

commit v5 on v4

--- a/solution.py
+++ b/solution.py
@@ -17,7 +17,7 @@
         return [1] * per
     unit = per // 8
     tail = max(1, 3 * unit // 4)
-    return [2 * unit] * 2 + [2 * unit - tail] * 2 + [tail] * 2 if last else [4 * unit] * 2
+    return [2 * unit] * 2 + [2 * unit - tail] * 2 + [tail] * 2 if last else [unit] * 2 + [3 * unit] * 2
 
 
 def layout(mesh, shape, n_slab):
@@ -54,7 +54,9 @@
         del scratch[:n]
         return out
 
-    g, totals = take(ntab), take(ntab)
+    g = [take(2) for _ in range(ntab)]
+    totals = take(ntab)
+    half = width // 2
     sq = take(n_pieces)
     (ids_v, order_v, code_v, order_s, code_s, packed, landed, relayed, arrived, acc_slot, step, sent, spare,
      in_sem, meta_sem, send_sem, far_sem, own_sem, sq_sem, up, down, spare_sem) = scratch
@@ -66,8 +68,9 @@
 
     ids_copy = pltpu.make_async_copy(ids_hbm, ids_v, in_sem.at[0])
     ids_copy.start()
-    grad_copies = [pltpu.make_async_copy(grads_hbm.at[0, t], g[t], in_sem.at[3 + t]) for t in range(ntab)]
-    for copy in grad_copies:
+    grad_copies = [[pltpu.make_async_copy(grads_hbm.at[0, t, pl.ds(h * half, half)], g[t][h], in_sem.at[3 + 2 * t + h])
+                    for h in range(2)] for t in range(ntab)]
+    for copy in grad_copies[0]:
         copy.start()
 
     barrier = pltpu.get_barrier_semaphore()
@@ -83,9 +86,7 @@
     pl.when(my_col < cols - 1)(lambda: pass_on(barrier, 1))
 
     acc_copy = pltpu.make_async_copy(acc_hbm, new_acc, in_sem.at[1])
-    acc_copy.start()
     table_copy = pltpu.make_async_copy(tables_hbm, image, in_sem.at[2])
-    table_copy.start()
 
     lane = lax.broadcasted_iota(jnp.int32, (nblk, nblk), 1)
     slot = lax.broadcasted_iota(jnp.int32, (nblk, nblk), 0)
@@ -100,22 +101,26 @@
 
     def rank_blocks(t):
         across = jnp.broadcast_to(ids_v[pl.ds(t, 1), :], (nblk, nblk))
-        down = across.T
-        place = jnp.sum(jnp.where(down < across, 1, 0), axis=0, keepdims=True)
+        column = across.T
+        place = jnp.sum(jnp.where(column < across, 1, 0), axis=0, keepdims=True)
         hit = jnp.broadcast_to(place, (nblk, nblk)).T == lane
         order = jnp.sum(jnp.where(hit, slot, 0), axis=0, keepdims=True)
-        block = jnp.sum(jnp.where(hit, down, 0), axis=0, keepdims=True) - me * local
-        order_v[t, pl.ds(0, 1), :] = jnp.clip(order, 0, nblk - 1)
+        block = jnp.sum(jnp.where(hit, column, 0), axis=0, keepdims=True) - me * local
+        order = jnp.clip(order, 0, nblk - 1)
+        order_v[t, pl.ds(0, 1), :] = order
         order_v[t, pl.ds(1, 1), :] = jnp.clip(block, 0, local - 1)
         order_copy(t).start()
-        col = jnp.broadcast_to(down[:, :1], (nblk, wide))
+        return order, column
+
+    def rank_local(t, column):
+        col = jnp.broadcast_to(column[:, :1], (nblk, wide))
         below = jnp.sum(jnp.where(col < own_block, 1, 0), axis=0, keepdims=True) - me * per
         found = jnp.sum(jnp.where(col == own_block, 1, 0), axis=0, keepdims=True)
         code_v[t, pl.ds(0, 1), :] = jnp.where(found > 0, jnp.clip(below, 0, per - 1), -1)
         code_copy(t).start()
 
     ids_copy.wait()
-    rank_blocks(0)
+    first_order, column = rank_blocks(0)
 
     def axes(p):
         return (inner, outer) if p % 2 == 0 else (outer, inner)
@@ -130,8 +135,8 @@
         return pl.ds(t * per + start, n)
 
     def mine(t, owner, i):
-        at = order_s[t, 0, owner * per + i]
-        return g[t][:, lanes(at)].astype(jnp.float32)
+        where = lanes(order_s[t, 0, owner * per + i])
+        return jnp.concatenate([part[:, where].astype(jnp.float32) for part in g[t]], axis=0)
 
     def first_copy(p, f, s):
         here = arrived.at[f - 1, span(p)] if s == 0 else landed.at[f - 1, s - 1, span(p)]
@@ -195,6 +200,29 @@
 
         pl.when((way(p, owner) != d) if relaying else (way(p, owner) == d))(send)
 
+    def first_far(p, picked, h):
+        t, start, n = pieces[p]
+        nf, ns = axes(p)
+        dims = pl.ds(h * half, half)
+        for s in range(1, ns):
+            for f in range(1, nf):
+                for i in range(n):
+                    block = g[t][h][:, lanes(picked[f, s][i])].astype(jnp.float32)
+                    packed[f - 1, s, t * per + start + i, dims] = block
+                pltpu.make_async_remote_copy(
+                    packed.at[f - 1, s, span(p), dims], landed.at[f - 1, s - 1, span(p), dims],
+                    send_sem.at[0], far_sem.at[p], device_id={"rep": rank(p, f, 0)}, device_id_type=MESH).start()
+
+    def pick(p):
+        _, start, n = pieces[p]
+        nf, ns = axes(p)
+        picked = {}
+        for s in range(1, ns):
+            for f in range(1, nf):
+                row = pltpu.roll(first_order, lax.rem(nblk - rank(p, f, s) * per, nblk), 1)
+                picked[f, s] = [row[0, start + i] for i in range(n)]
+        return picked
+
     def send_far(p):
         if p >= first_steered:
             steered_far(p)
@@ -269,17 +297,26 @@
         pl.when(behind)(lambda: pl.semaphore_wait(sem, 1))
         pl.when(ahead)(lambda: pass_on(sem, way))
 
+    picked = [pick(p) for p in range(2)]
+    beside = jnp.minimum(my_col, 1) + jnp.minimum(cols - 1 - my_col, 1)
+    pl.semaphore_wait(barrier, inner - 1 + outer - 1 + beside)
+    for h in range(2):
+        grad_copies[0][h].wait()
+        for p in range(2):
+            first_far(p, picked[p], h)
+    for copy in [*sum(grad_copies[1:], []), acc_copy, table_copy]:
+        copy.start()
     for t in range(ntab):
+        if t > 0:
+            for copy in grad_copies[t]:
+                copy.wait()
         order_copy(t).wait()
-        grad_copies[t].wait()
-        if t == 0:
-            beside = jnp.minimum(my_col, 1) + jnp.minimum(cols - 1 - my_col, 1)
-            pl.semaphore_wait(barrier, inner - 1 + outer - 1 + beside)
-        for p in range(n_pieces):
+        for p in range(2, n_pieces):
             if pieces[p][0] == t:
                 send_far(p)
+        rank_local(t, column)
         if t + 1 < ntab:
-            rank_blocks(t + 1)
+            column = rank_blocks(t + 1)[1]
     for p in range(n_pieces):
         send_near(p)
 
@@ -342,7 +379,7 @@
         in_specs=[hbm] * 4,
         out_specs=(vmem, vmem),
         scratch_shapes=[
-            *[pltpu.VMEM(replica_grads.shape[2:], replica_grads.dtype) for _ in range(ntab)],
+            *[pltpu.VMEM((width // 2, replica_grads.shape[3]), replica_grads.dtype) for _ in range(2 * ntab)],
             *[pltpu.VMEM((per, width, BLOCK), f32) for _ in range(ntab)],
             *[pltpu.VMEM((cols, n, BLOCK), f32) for _, _, n in pieces],
             pltpu.VMEM(block_ids.shape, i32),
@@ -358,7 +395,7 @@
             pltpu.VMEM((ntab, per, BLOCK), f32),
             pltpu.VMEM((cols - 1, slots, BLOCK), f32),
             pltpu.VMEM((2, 2, pieces[-1][2], width, BLOCK), f32),
-            dma((3 + ntab,)), dma((2, ntab)), dma((3,)),
+            dma((3 + 2 * ntab,)), dma((2, ntab)), dma((3,)),
             dma((n_pieces,)), dma((n_pieces,)), dma((n_pieces,)),
             pltpu.SemaphoreType.REGULAR, pltpu.SemaphoreType.REGULAR, dma((2, 2)),
         ],

time: 45.9 us -> 45.7 us (level)
  no operation moved by 1% of the time
where the time goes in v5:
time: 45.7 us; the launch traced here: 45.5 us
  Pallas kernels  44.9 us (98%)
  between operations  0.64 us (1%)
    pallas_call x1, Pallas kernels, body(): pl.pallas_call(functools.partial(step_kernel, cfg), out_shape=(jax.ShapeD...  43.5 us
    pallas_call x1, Pallas kernels, body(): pl.pallas_call(store_kernel, out_shape=(jax.ShapeDtypeStruct(tables.shape...  1.37 us

profile of v5, /device:TPU:0, one launch (start us, length us, event | category | flops | bytes accessed | tf_op | source)
XLA Modules:
  0.0 45.5 jit_solution(8929256296280040272)
XLA Ops:
  0.6 43.5 %exchange.1 = (f32[2,32,8192]{2,1,0:T(8,128)S(1)}, f32[2,8192]{1,0:T(2,128)S(1)}) custom-call(s32[2,128]{1,0:T(2,128)} %ids_hbm.1, bf16[1,2,32,16384]{3,2,1,0:T(8,128)(2,1)} %grads_hbm.1, f32[2,32,8192]{2,1,0:T(8,128)} %tables_hbm.1, f32[2,8192]{1,0:T(2,128)} %acc_hbm.1), custom_call_target="tpu_custom_call" | custom-call | tf_op jit(solution)/shard_map/exchange/pallas_call | solution.py:376
  44.1 1.4 %store.1 = (f32[2,32,8192]{2,1,0:T(8,128)}, f32[2,8192]{1,0:T(2,128)}) custom-call(f32[2,32,8192]{2,1,0:T(8,128)S(1)} %get-tuple-element.4.image, f32[2,8192]{1,0:T(2,128)S(1)} %get-tuple-element.5.acc), custom_call_target="tpu_custom_call" | custom-call | tf_op jit(solution)/shard_map/store/pallas_call | solution.py:406

commit v6 on v5

--- a/solution.py
+++ b/solution.py
@@ -94,10 +94,10 @@
     own_block = lax.broadcasted_iota(jnp.int32, (nblk, wide), 1) + me * local
 
     def order_copy(t):
-        return pltpu.make_async_copy(order_v.at[t], order_s.at[t], meta_sem.at[0, t])
+        return pltpu.make_async_copy(order_v.at[t], order_s.at[t], meta_sem.at[t])
 
     def code_copy(t):
-        return pltpu.make_async_copy(code_v.at[t], code_s.at[t], meta_sem.at[1, t])
+        return pltpu.make_async_copy(code_v.at[t], code_s.at[t], meta_sem.at[ntab])
 
     def rank_blocks(t):
         across = jnp.broadcast_to(ids_v[pl.ds(t, 1), :], (nblk, nblk))
@@ -150,9 +150,13 @@
             relayed.at[s - 1, span(p)], arrived.at[nf - 2 + s, span(p)], send_sem.at[1], own_sem.at[p],
             device_id={"rep": rank(p, 0, s)}, device_id_type=MESH)
 
+    def square_slot(p):
+        t = pieces[p][0]
+        return t if t < ntab - 1 else t + sum(q[0] == t for q in pieces[:p])
+
     def square_copy(p, f):
         return pltpu.make_async_remote_copy(
-            sq[p].at[my_col], sq[p].at[my_col], send_sem.at[2], sq_sem.at[p],
+            sq[p].at[my_col], sq[p].at[my_col], send_sem.at[2], sq_sem.at[square_slot(p)],
             device_id={"col": lax.rem(my_col + f, cols)}, device_id_type=MESH)
 
     def wait_all(ref, sem):
@@ -272,7 +276,10 @@
 
     def gather(p):
         t, start, n = pieces[p]
-        wait_all(sq[p].at[pl.ds(0, cols - 1)], sq_sem.at[p])
+        if t == ntab - 1:
+            wait_all(sq[p].at[pl.ds(0, cols - 1)], sq_sem.at[square_slot(p)])
+        elif start == 0:
+            wait_all(sent.at[:, pl.ds(0, per)], sq_sem.at[square_slot(p)])
         acc = sq[p][0]
         for f in range(1, cols):
             acc = acc + sq[p][f]
@@ -282,12 +289,13 @@
         for i in range(start, start + n):
             totals[t][i] = totals[t][i] * step[t, pl.ds(i, 1), :]
 
-    def place(t):
-        for b in range(local):
+    def place(t, first, end):
+        for b in range(first, min(local, local - per + end)):
             code = code_s[t, 0, b]
             at = jnp.maximum(code, 0)
             where = pl.ds(b * BLOCK, BLOCK)
-            hit = jnp.full((width, BLOCK), code, jnp.int32) >= 0
+            spread = jnp.full((width, BLOCK), code, jnp.int32)
+            hit = (spread >= first) & (spread < end) if end < per else spread >= first
             old = image[t, :, where]
             image[t, :, where] = jnp.where(hit, old - totals[t][at], old)
             old_acc = new_acc[pl.ds(t, 1), where]
@@ -331,15 +339,16 @@
     sweep(up, 1, my_col > 0, my_col < cols - 1)
     sweep(down, -1, my_col < cols - 1, my_col > 0)
     table_copy.wait()
-    for t in range(ntab):
-        code_copy(t).wait()
+    wait_all(code_v, meta_sem.at[ntab])
     for p in range(n_pieces):
         finish(p)
+    placed = 0
     for p in range(n_pieces):
         gather(p)
-        t = pieces[p][0]
-        if p + 1 == n_pieces or pieces[p + 1][0] != t:
-            place(t)
+        t, start, n = pieces[p]
+        if start + n == per or p == n_pieces - 3:
+            place(t, placed, start + n)
+            placed = 0 if start + n == per else start + n
 
     if inner == outer:
         wait_all(packed, send_sem.at[0])
@@ -395,8 +404,8 @@
             pltpu.VMEM((ntab, per, BLOCK), f32),
             pltpu.VMEM((cols - 1, slots, BLOCK), f32),
             pltpu.VMEM((2, 2, pieces[-1][2], width, BLOCK), f32),
-            dma((3 + 2 * ntab,)), dma((2, ntab)), dma((3,)),
-            dma((n_pieces,)), dma((n_pieces,)), dma((n_pieces,)),
+            dma((3 + 2 * ntab,)), dma((ntab + 1,)), dma((3,)),
+            dma((n_pieces - cfg["steered"],)), dma((n_pieces,)), dma((ntab - 1 + sum(q[0] == ntab - 1 for q in pieces),)),
             pltpu.SemaphoreType.REGULAR, pltpu.SemaphoreType.REGULAR, dma((2, 2)),
         ],
         compiler_params=pltpu.CompilerParams(

time: 45.7 us -> 45.6 us (level)
  no operation moved by 1% of the time
where the time goes in v6:
time: 45.6 us; the launch traced here: 45.4 us
  Pallas kernels  44.8 us (98%)
  between operations  0.64 us (1%)
    pallas_call x1, Pallas kernels, body(): pl.pallas_call(functools.partial(step_kernel, cfg), out_shape=(jax.ShapeD...  43.4 us
    pallas_call x1, Pallas kernels, body(): pl.pallas_call(store_kernel, out_shape=(jax.ShapeDtypeStruct(tables.shape...  1.37 us

profile of v6, /device:TPU:0, one launch (start us, length us, event | category | flops | bytes accessed | tf_op | source)
XLA Modules:
  0.0 45.4 jit_solution(6976468188411027127)
XLA Ops:
  0.6 43.4 %exchange.1 = (f32[2,32,8192]{2,1,0:T(8,128)S(1)}, f32[2,8192]{1,0:T(2,128)S(1)}) custom-call(s32[2,128]{1,0:T(2,128)} %ids_hbm.1, bf16[1,2,32,16384]{3,2,1,0:T(8,128)(2,1)} %grads_hbm.1, f32[2,32,8192]{2,1,0:T(8,128)} %tables_hbm.1, f32[2,8192]{1,0:T(2,128)} %acc_hbm.1), custom_call_target="tpu_custom_call" | custom-call | tf_op jit(solution)/shard_map/exchange/pallas_call | solution.py:385
  44.0 1.4 %store.1 = (f32[2,32,8192]{2,1,0:T(8,128)}, f32[2,8192]{1,0:T(2,128)}) custom-call(f32[2,32,8192]{2,1,0:T(8,128)S(1)} %get-tuple-element.4.image, f32[2,8192]{1,0:T(2,128)S(1)} %get-tuple-element.5.acc), custom_call_target="tpu_custom_call" | custom-call | tf_op jit(solution)/shard_map/store/pallas_call | solution.py:415

commit v7 on v6

--- a/solution.py
+++ b/solution.py
@@ -141,18 +141,21 @@
     def first_copy(p, f, s):
         here = arrived.at[f - 1, span(p)] if s == 0 else landed.at[f - 1, s - 1, span(p)]
         return pltpu.make_async_remote_copy(
-            packed.at[f - 1, s, span(p)], here, send_sem.at[0], own_sem.at[p] if s == 0 else far_sem.at[p],
+            packed.at[f - 1, s, span(p)], here, send_sem.at[0], own_sem.at[own_slot(p)] if s == 0 else far_sem.at[p],
             device_id={"rep": rank(p, f, 0)}, device_id_type=MESH)
 
     def second_copy(p, s):
         nf = axes(p)[0]
         return pltpu.make_async_remote_copy(
-            relayed.at[s - 1, span(p)], arrived.at[nf - 2 + s, span(p)], send_sem.at[1], own_sem.at[p],
+            relayed.at[s - 1, span(p)], arrived.at[nf - 2 + s, span(p)], send_sem.at[1], own_sem.at[own_slot(p)],
             device_id={"rep": rank(p, 0, s)}, device_id_type=MESH)
 
     def square_slot(p):
         t = pieces[p][0]
         return t if t < ntab - 1 else t + sum(q[0] == t for q in pieces[:p])
+
+    def own_slot(p):
+        return square_slot(p) if inner == outer else p
 
     def square_copy(p, f):
         return pltpu.make_async_remote_copy(
@@ -199,7 +202,7 @@
                     acc = acc + spare[1 - d, b, i]
                 out[t * per + start + i] = acc
             pltpu.make_async_remote_copy(
-                out.at[span(p)], arrived.at[d, span(p)], send_sem.at[d], own_sem.at[p],
+                out.at[span(p)], arrived.at[d, span(p)], send_sem.at[d], own_sem.at[own_slot(p)],
                 device_id={"rep": owner}, device_id_type=MESH).start()
 
         pl.when((way(p, owner) != d) if relaying else (way(p, owner) == d))(send)
@@ -264,7 +267,10 @@
     def finish(p):
         t, start, n = pieces[p]
         nf, ns = axes(p)
-        wait_all(arrived.at[pl.ds(0, nf + ns - 2), span(p)], own_sem.at[p])
+        if t == ntab - 1 or inner != outer:
+            wait_all(arrived.at[pl.ds(0, nf + ns - 2), span(p)], own_sem.at[own_slot(p)])
+        elif start == 0:
+            wait_all(arrived.at[pl.ds(0, nf + ns - 2), pl.ds(t * per, per)], own_sem.at[own_slot(p)])
         for i in range(n):
             acc = mine(t, me, start + i)
             for k in range(nf + ns - 2):
@@ -377,6 +383,7 @@
     cols, pieces = cfg["cols"], cfg["pieces"]
     side = max(cfg["inner"], cfg["outer"])
     slots, n_pieces = ntab * per, len(pieces)
+    few = ntab - 1 + sum(q[0] == ntab - 1 for q in pieces)
     wide = -(-cfg["local"] // BLOCK) * BLOCK
     f32, i32 = jnp.float32, jnp.int32
     dma = pltpu.SemaphoreType.DMA
@@ -405,7 +412,7 @@
             pltpu.VMEM((cols - 1, slots, BLOCK), f32),
             pltpu.VMEM((2, 2, pieces[-1][2], width, BLOCK), f32),
             dma((3 + 2 * ntab,)), dma((ntab + 1,)), dma((3,)),
-            dma((n_pieces - cfg["steered"],)), dma((n_pieces,)), dma((ntab - 1 + sum(q[0] == ntab - 1 for q in pieces),)),
+            dma((n_pieces - cfg["steered"],)), dma((few if cfg["inner"] == cfg["outer"] else n_pieces,)), dma((few,)),
             pltpu.SemaphoreType.REGULAR, pltpu.SemaphoreType.REGULAR, dma((2, 2)),
         ],
         compiler_params=pltpu.CompilerParams(

time: 45.6 us -> 45.5 us (level)
  no operation moved by 1% of the time
where the time goes in v7:
time: 45.5 us; the launch traced here: 45.4 us
  Pallas kernels  44.7 us (98%)
  between operations  0.64 us (1%)
    pallas_call x1, Pallas kernels, body(): pl.pallas_call(functools.partial(step_kernel, cfg), out_shape=(jax.ShapeD...  43.4 us
    pallas_call x1, Pallas kernels, body(): pl.pallas_call(store_kernel, out_shape=(jax.ShapeDtypeStruct(tables.shape...  1.37 us

profile of v7, /device:TPU:0, one launch (start us, length us, event | category | flops | bytes accessed | tf_op | source)
XLA Modules:
  0.0 45.4 jit_solution(17881540688669065093)
XLA Ops:
  0.6 43.4 %exchange.1 = (f32[2,32,8192]{2,1,0:T(8,128)S(1)}, f32[2,8192]{1,0:T(2,128)S(1)}) custom-call(s32[2,128]{1,0:T(2,128)} %ids_hbm.1, bf16[1,2,32,16384]{3,2,1,0:T(8,128)(2,1)} %grads_hbm.1, f32[2,32,8192]{2,1,0:T(8,128)} %tables_hbm.1, f32[2,8192]{1,0:T(2,128)} %acc_hbm.1), custom_call_target="tpu_custom_call" | custom-call | tf_op jit(solution)/shard_map/exchange/pallas_call | solution.py:392
  44.0 1.4 %store.1 = (f32[2,32,8192]{2,1,0:T(8,128)}, f32[2,8192]{1,0:T(2,128)}) custom-call(f32[2,32,8192]{2,1,0:T(8,128)S(1)} %get-tuple-element.4.image, f32[2,8192]{1,0:T(2,128)S(1)} %get-tuple-element.5.acc), custom_call_target="tpu_custom_call" | custom-call | tf_op jit(solution)/shard_map/store/pallas_call | solution.py:422
